TPU v7x, 32 devices: a whole 2x2x4 slice. The times are simulated.
32 devices in a mesh: kgrp: 4 (over x, core), tile: 8 (over z, y).
Axes of the slice: x: 2, y: 2, z: 4, core: 2. Of those that a mesh axis runs over, the one named last changes fastest.
Arguments:
- mask_spectrum: float32 [32, 2, 512, 512], P(('kgrp', 'tile')), may hold values from -6 to 6
- kernels: float32 [8, 2, 512, 512], P('kgrp', None, 'tile'), may hold values from -6 to 6
- owner_table: int32 [4], replicated, may hold values from 0 to 7
- step_weight: float32 [4], replicated, may hold values from 0.25 to 1
Outputs:
- intensity: float32 [32, 512, 512], P(('kgrp', 'tile'))
Inputs may be any that keep to these rules, and one draw needn't show every extreme that they name: `owner_table`: kernel indices, possibly repeated across steps.
All inputs are finite; a program needn't handle non-finite values.
Results may differ from a plain program's by a relative error of at most 0.0001.
Values sent between devices are 32-bit elements; how exact they have to be, the bound alone decides.
A program may use at most 128 MiB of HBM per device.

v0:
```python
import functools
import math

import jax
import jax.numpy as jnp
import ml_dtypes
import numpy as np
from jax import lax
from jax.experimental import pallas as pl
from jax.experimental.pallas import tpu as pltpu
from jax.sharding import PartitionSpec as P

MESH = pl.DeviceIdType.MESH
BF = jnp.bfloat16
F32 = jnp.float32


def split_np(x):
    hi = x.astype(np.float32).astype(ml_dtypes.bfloat16)
    lo = (x - hi.astype(np.float64)).astype(np.float32).astype(ml_dtypes.bfloat16)
    return hi, lo


def tables(n, radix):
    m = n // radix
    a = np.arange(m)
    rows = []
    for r in range(radix):
        phase = (a[:, None] * (r + radix * a[None, :])) % n * (2.0 * math.pi / n)
        c, s = np.cos(phase) / math.sqrt(n), np.sin(phase) / math.sqrt(n)
        rows.append(np.block([[c, s], [-s, c]]))
    b = np.stack(rows)
    bh, bl = split_np(b)
    row = np.concatenate([bh, bl], axis=1)
    col = np.concatenate([bh.transpose(0, 2, 1), bl.transpose(0, 2, 1)], axis=2)
    return row, col


def split(x):
    hi = x.astype(BF)
    return hi, (x - hi.astype(F32)).astype(BF)


def radix4(re, im):
    ar, ai, br, bi = re[0] + re[2], im[0] + im[2], re[0] - re[2], im[0] - im[2]
    cr, ci, dr, di = re[1] + re[3], im[1] + im[3], re[1] - re[3], im[1] - im[3]
    return [(ar + cr, ai + ci), (br - di, bi + dr), (ar - cr, ai - ci), (br + di, bi - dr)]


def kernel(dims, owner_ref, weight_ref, mask_hbm, kern_hbm, rowt_hbm, colt_hbm, out_ref,
           held, cand, mask, rowt, colt, lane_perm, stage, field, cols, total, blocks,
           z_send, z_recv, x_send, x_recv, y_send, y_recv, d_send, d_recv,
           c_send, c_recv, k_send, k_recv, loc):
    steps, groups, nk, nz, rows, n, m = dims
    g = lax.axis_index("kgrp")
    t = lax.axis_index("tile")
    x, c = g // 2, g % 2
    xo, co = 1 - x, 1 - c
    z, y = t // 2, t % 2
    yo = 1 - y
    x_peer, c_peer = {"kgrp": 2 * xo + c}, {"kgrp": 2 * x + co}
    y_peer = {"tile": 2 * z + yo}
    d_peer = {"kgrp": 2 * (x * (1 - c) + xo * c) + c, "tile": 2 * z + yo * (1 - c) + y * c}
    d_q = 2 * (xo * (1 - c) + x * c) + c
    d_y = y * (1 - c) + yo * c

    loads = [
        pltpu.make_async_copy(kern_hbm.at[:, :, :, pl.ds(pl.multiple_of(g * m, m), m)], cand.at[pl.ds(g * nk, nk)], loc.at[0]),
        pltpu.make_async_copy(mask_hbm, mask, loc.at[1]),
        pltpu.make_async_copy(rowt_hbm, rowt, loc.at[2]),
        pltpu.make_async_copy(colt_hbm, colt, loc.at[3]),
    ]
    for load in loads:
        load.start()

    barrier = pltpu.get_barrier_semaphore()
    for d in range(1, groups):
        pl.semaphore_signal(barrier, inc=1, device_id={"kgrp": (g + d) % groups}, device_id_type=MESH)
    pl.semaphore_signal(barrier, inc=1, device_id=y_peer, device_id_type=MESH)
    for d in range(1, nz):
        pl.semaphore_signal(barrier, inc=1, device_id={"tile": 2 * ((z + d) % nz) + y}, device_id_type=MESH)
    pl.semaphore_wait(barrier, groups + nz - 1)

    sent = []

    def send(src, dst, send_sem, recv_sem, device):
        copy = pltpu.make_async_remote_copy(src_ref=src, dst_ref=dst, send_sem=send_sem, recv_sem=recv_sem,
                                            device_id=device, device_id_type=MESH)
        copy.start()
        sent.append(copy)

    def arrive(ref, recv_sem):
        pltpu.make_async_remote_copy(src_ref=ref, dst_ref=ref, send_sem=recv_sem, recv_sem=recv_sem,
                                     device_id=c_peer, device_id_type=MESH).wait_recv()

    for d in range(1, groups):
        peer = (g + d) % groups
        send(kern_hbm.at[:, :, :, pl.ds(pl.multiple_of(peer * m, m), m)], cand.at[pl.ds(g * nk, nk)],
             k_send.at[d - 1], k_recv.at[d - 1], {"kgrp": peer})

    src_lane = lax.broadcasted_iota(jnp.int32, (n, n), 0)
    dst_lane = lax.broadcasted_iota(jnp.int32, (n, n), 1)
    radix = n // m
    lane_perm[...] = jnp.where((src_lane % m) * radix + src_lane // m == dst_lane, 1.0, 0.0).astype(BF)

    loads[0].wait()
    for d in range(1, groups):
        arrive(cand.at[pl.ds(((g + groups - d) % groups) * nk, nk)], k_recv.at[d - 1])
    for s in range(steps):
        held[s, g, :, z, y] = cand[owner_ref[s]]

    def near(d):
        return (z + d) % nz

    def piece(s, q, zz, yy):
        return held.at[s, q, :, zz, yy]

    def line(s, q, yy):
        return held.at[s, q, :, :, yy]

    def cross(s, d):
        own = piece(s, g, near(d), y)
        send(own, own, x_send.at[s, d], x_recv.at[s, d], x_peer)
        send(own, own, y_send.at[s, d], y_recv.at[s, d], y_peer)

    def to_core(s, kind, q, yy):
        send(line(s, q, yy), line(s, q, yy), c_send.at[s, kind], c_recv.at[s, kind], c_peer)

    def gather_z(s):
        for d in range(1, nz):
            arrive(piece(s, g, near(nz - d), y), z_recv.at[s, d])
            cross(s, nz - d)
        to_core(s, 0, g, y)

    def gather_xy(s):
        for d in [0] + [nz - d for d in range(1, nz)]:
            arrive(piece(s, 2 * xo + c, near(d), y), x_recv.at[s, d])
            arrive(piece(s, g, near(d), yo), y_recv.at[s, d])
            turned = piece(s, d_q, near(d), d_y)
            send(turned, turned, d_send.at[s, d], d_recv.at[s, d], d_peer)
        to_core(s, 1, 2 * xo + c, y)
        to_core(s, 2, g, yo)

    def gather_rest(s):
        for d in range(nz):
            arrive(piece(s, 2 * xo + c, near(d), yo), d_recv.at[s, d])
        to_core(s, 3, 2 * xo + c, yo)
        for kind, (q, yy) in enumerate([(2 * x + co, y), (2 * xo + co, y), (2 * x + co, yo), (2 * xo + co, yo)]):
            arrive(line(s, q, yy), c_recv.at[s, kind])

    def compute(s):
        @pl.loop(0, 2 * nz)
        def _(i):
            at = pl.ds(pl.multiple_of(i * rows, rows), rows)
            re, im = [], []
            for q in range(groups):
                kr, ki = held[s, q, 0, i // 2, i % 2], held[s, q, 1, i // 2, i % 2]
                mr, mi = mask[0, at, q * m:(q + 1) * m], mask[1, at, q * m:(q + 1) * m]
                re.append(mr * kr - mi * ki)
                im.append(mr * ki + mi * kr)
            for r, (pr, pi) in enumerate(radix4(re, im)):
                for p, part in enumerate((pr, pi)):
                    hi, lo = split(part)
                    stage[r, at, p * m:(p + 1) * m] = hi
                    stage[r, at, (2 + p) * m:(3 + p) * m] = lo

        for r in range(radix):
            hi, lo = stage[r, :, :2 * m], stage[r, :, 2 * m:]
            th, tl = rowt[r, :2 * m], rowt[r, 2 * m:]
            field[r] = jnp.dot(jnp.concatenate([hi, lo, hi], 1), jnp.concatenate([th, th, tl], 0),
                               preferred_element_type=F32)

        half = m // 4
        for ry in range(radix):
            @pl.loop(0, 4)
            def _(i):
                base = pl.multiple_of(i * half, half)
                re = [field[ry, pl.ds(k * m + base, half), :m] for k in range(radix)]
                im = [field[ry, pl.ds(k * m + base, half), m:] for k in range(radix)]
                for rx, parts in enumerate(radix4(re, im)):
                    for p, part in enumerate(parts):
                        hi, lo = split(part)
                        cols[rx, pl.ds(p * m + base, half), ry * m:(ry + 1) * m] = hi
                        cols[rx, pl.ds((2 + p) * m + base, half), ry * m:(ry + 1) * m] = lo

        for rx in range(radix):
            hi, lo = cols[rx, :2 * m], cols[rx, 2 * m:]
            th, tl = colt[rx, :, :2 * m], colt[rx, :, 2 * m:]
            done = jnp.dot(jnp.concatenate([th, th, tl], 1), jnp.concatenate([hi, lo, hi], 0),
                           preferred_element_type=F32)
            power = (done[:m] * done[:m] + done[m:] * done[m:]) * weight_ref[s]
            if s == 0:
                total[rx] = power
            else:
                total[rx] += power

    for s in range(steps):
        own = piece(s, g, z, y)
        for d in range(1, nz):
            send(own, own, z_send.at[s, d], z_recv.at[s, d], {"tile": 2 * near(d) + y})
        cross(s, 0)
    for load in loads[1:]:
        load.wait()
    gather_z(0)
    for s in range(steps):
        if s + 1 < steps:
            gather_z(s + 1)
        gather_xy(s)
        if s:
            gather_rest(s - 1)
            compute(s - 1)
    gather_rest(steps - 1)
    compute(steps - 1)

    for rx in range(radix):
        hi, lo = split(total[rx])
        perm = lane_perm[...]
        image = jnp.dot(jnp.concatenate([hi, lo], 1), jnp.concatenate([perm, perm], 0), preferred_element_type=F32)
        for q in range(radix):
            blocks[q, pl.ds(rx, m, stride=radix), :] = image[:, q * m:(q + 1) * m]
    for q in range(radix):
        out_ref[:, q * m:(q + 1) * m] = blocks[q]
    for copy in sent:
        copy.wait_send()


def local(mesh_shape, mask_spectrum, kernels, owner_table, step_weight):
    groups, tiles = mesh_shape
    nk, _, rows, n = kernels.shape
    steps = owner_table.shape[0]
    m = n // groups
    radix = groups
    nz = tiles // 2
    rowt, colt = tables(n, radix)
    dma = pltpu.SemaphoreType.DMA
    any_spec = pl.BlockSpec(memory_space=pl.ANY)
    smem = pl.BlockSpec(memory_space=pltpu.SMEM)
    out = pl.pallas_call(
        functools.partial(kernel, (steps, groups, nk, nz, rows, n, m)),
        out_shape=jax.ShapeDtypeStruct((n, n), F32),
        in_specs=[smem, smem, any_spec, any_spec, any_spec, any_spec],
        out_specs=pl.BlockSpec(memory_space=pltpu.VMEM),
        scratch_shapes=[
            pltpu.VMEM((steps, groups, 2, nz, 2, rows, m), F32),
            pltpu.VMEM((groups * nk, 2, rows, m), F32),
            pltpu.VMEM((2, n, n), F32),
            pltpu.VMEM(rowt.shape, BF),
            pltpu.VMEM(colt.shape, BF),
            pltpu.VMEM((n, n), BF),
            pltpu.VMEM((radix, n, 4 * m), BF),
            pltpu.VMEM((radix, n, 2 * m), F32),
            pltpu.VMEM((radix, 4 * m, n), BF),
            pltpu.VMEM((radix, m, n), F32),
            pltpu.VMEM((radix, n, m), F32),
        ] + [dma((steps, nz))] * 8 + [dma((steps, 4))] * 2 + [dma((groups - 1,))] * 2 + [dma((4,))],
        compiler_params=pltpu.CompilerParams(collective_id=0, has_side_effects=True, vmem_limit_bytes=62 * 1024 * 1024),
    )(owner_table, step_weight, mask_spectrum[0], kernels, jnp.asarray(rowt), jnp.asarray(colt))
    return out[None]


def solution(mesh):
    in_specs = (P(("kgrp", "tile"), None, None, None), P("kgrp", None, "tile", None), P(), P())
    out_specs = P(("kgrp", "tile"), None, None)
    body = functools.partial(local, (mesh.shape["kgrp"], mesh.shape["tile"]))
    return jax.shard_map(body, mesh=mesh, in_specs=in_specs, out_specs=out_specs, check_vma=False)
```

profile of v0, /device:TPU:11, one launch (start us, length us, event | category | flops | bytes accessed | tf_op | source)
XLA Modules:
  0.0 65.1 jit_solution(18285677523856897776)
XLA Ops:
  0.0 62.9 %shard_map.64 = f32[512,512]{1,0:T(8,128)} custom-call(s32[4]{0:T(128)} %owner_ref.1, f32[4]{0:T(128)} %weight_ref.1, f32[2,512,512]{2,1,0:T(8,128)} %bitcast.3, f32[2,2,64,512]{3,2,1,0:T(8,128)} %kern_hbm.1, bf16[4,512,256]{2,1,0:T(8,128)(2,1)} %constant.4.clone.rowt_hbm, bf16[4,256,512]{2,1,0:T(8,128)(2,1)} %constant.5.clone.colt_hbm), custom_call_target="tpu_custom_call" | custom-call | tf_op jit(solution)/shard_map/pallas_call | solution.py:238
  62.9 2.3 %copy.8 = f32[1,512,512]{2,1,0:T(8,128)} copy(f32[1,512,512]{2,1,0:T(8,128)} %bitcast.2) | data formatting | bytes 2097152
where the time goes:
time: 65.3 us; the launch traced here: 65.1 us
  Pallas kernels  62.9 us (96%)
  local copies, waits for them, and re-layouts  2.26 us (3%)
    pallas_call x1, Pallas kernels, local(): pl.pallas_call(functools.partial(kernel, (steps, groups, nk, nz, rows, n,...  62.9 us
    unnamed x1, local copies, waits for them, and re-layouts  2.26 us

commit v1 on v0

--- a/solution.py
+++ b/solution.py
@@ -47,8 +47,8 @@
     return [(ar + cr, ai + ci), (br - di, bi + dr), (ar - cr, ai - ci), (br + di, bi - dr)]
 
 
-def kernel(dims, owner_ref, weight_ref, mask_hbm, kern_hbm, rowt_hbm, colt_hbm, out_ref,
-           held, cand, mask, rowt, colt, lane_perm, stage, field, cols, total, blocks,
+def kernel(dims, owner_ref, weight_ref, mask_hbm, kern_hbm, rowt_hbm, colt_hbm, total,
+           held, cand, mask, rowt, colt, stage, field, cols,
            z_send, z_recv, x_send, x_recv, y_send, y_recv, d_send, d_recv,
            c_send, c_recv, k_send, k_recv, loc):
     steps, groups, nk, nz, rows, n, m = dims
@@ -98,11 +98,7 @@
         send(kern_hbm.at[:, :, :, pl.ds(pl.multiple_of(peer * m, m), m)], cand.at[pl.ds(g * nk, nk)],
              k_send.at[d - 1], k_recv.at[d - 1], {"kgrp": peer})
 
-    src_lane = lax.broadcasted_iota(jnp.int32, (n, n), 0)
-    dst_lane = lax.broadcasted_iota(jnp.int32, (n, n), 1)
     radix = n // m
-    lane_perm[...] = jnp.where((src_lane % m) * radix + src_lane // m == dst_lane, 1.0, 0.0).astype(BF)
-
     loads[0].wait()
     for d in range(1, groups):
         arrive(cand.at[pl.ds(((g + groups - d) % groups) * nk, nk)], k_recv.at[d - 1])
@@ -212,16 +208,28 @@
     gather_rest(steps - 1)
     compute(steps - 1)
 
-    for rx in range(radix):
-        hi, lo = split(total[rx])
-        perm = lane_perm[...]
-        image = jnp.dot(jnp.concatenate([hi, lo], 1), jnp.concatenate([perm, perm], 0), preferred_element_type=F32)
-        for q in range(radix):
-            blocks[q, pl.ds(rx, m, stride=radix), :] = image[:, q * m:(q + 1) * m]
+    for copy in sent:
+        copy.wait_send()
+
+
+def order(dims, total, out_ref, lane_perm, blocks):
+    radix, m, n = dims
+    part = total.shape[1]
+
+    @pl.when(pl.program_id(0) == 0)
+    def _():
+        src_lane = lax.broadcasted_iota(jnp.int32, (n, n), 0)
+        dst_lane = lax.broadcasted_iota(jnp.int32, (n, n), 1)
+        lane_perm[...] = jnp.where((src_lane % m) * radix + src_lane // m == dst_lane, 1.0, 0.0).astype(BF)
+
+    hi, lo = split(total[...].reshape(radix * part, n))
+    perm = lane_perm[...]
+    image = jnp.dot(jnp.concatenate([hi, lo], 1), jnp.concatenate([perm, perm], 0), preferred_element_type=F32)
+    for q in range(radix):
+        for rx in range(radix):
+            blocks[q, pl.ds(rx, part, stride=radix), :] = image[rx * part:(rx + 1) * part, q * m:(q + 1) * m]
     for q in range(radix):
         out_ref[:, q * m:(q + 1) * m] = blocks[q]
-    for copy in sent:
-        copy.wait_send()
 
 
 def local(mesh_shape, mask_spectrum, kernels, owner_table, step_weight):
@@ -235,9 +243,9 @@
     dma = pltpu.SemaphoreType.DMA
     any_spec = pl.BlockSpec(memory_space=pl.ANY)
     smem = pl.BlockSpec(memory_space=pltpu.SMEM)
-    out = pl.pallas_call(
+    total = pl.pallas_call(
         functools.partial(kernel, (steps, groups, nk, nz, rows, n, m)),
-        out_shape=jax.ShapeDtypeStruct((n, n), F32),
+        out_shape=jax.ShapeDtypeStruct((radix, m, n), F32),
         in_specs=[smem, smem, any_spec, any_spec, any_spec, any_spec],
         out_specs=pl.BlockSpec(memory_space=pltpu.VMEM),
         scratch_shapes=[
@@ -246,15 +254,21 @@
             pltpu.VMEM((2, n, n), F32),
             pltpu.VMEM(rowt.shape, BF),
             pltpu.VMEM(colt.shape, BF),
-            pltpu.VMEM((n, n), BF),
             pltpu.VMEM((radix, n, 4 * m), BF),
             pltpu.VMEM((radix, n, 2 * m), F32),
             pltpu.VMEM((radix, 4 * m, n), BF),
-            pltpu.VMEM((radix, m, n), F32),
-            pltpu.VMEM((radix, n, m), F32),
         ] + [dma((steps, nz))] * 8 + [dma((steps, 4))] * 2 + [dma((groups - 1,))] * 2 + [dma((4,))],
         compiler_params=pltpu.CompilerParams(collective_id=0, has_side_effects=True, vmem_limit_bytes=62 * 1024 * 1024),
     )(owner_table, step_weight, mask_spectrum[0], kernels, jnp.asarray(rowt), jnp.asarray(colt))
+    part = m // 4
+    out = pl.pallas_call(
+        functools.partial(order, (radix, m, n)),
+        grid=(4,),
+        out_shape=jax.ShapeDtypeStruct((n, n), F32),
+        in_specs=[pl.BlockSpec((radix, part, n), lambda i: (0, i, 0))],
+        out_specs=pl.BlockSpec((radix * part, n), lambda i: (i, 0)),
+        scratch_shapes=[pltpu.VMEM((n, n), BF), pltpu.VMEM((radix, radix * part, m), F32)],
+    )(total)
     return out[None]
 
 

time: 65.3 us -> 66.5 us (1.018)
  Pallas kernels: 62.9 us -> 66.3 us
  local copies, waits for them, and re-layouts: 2.26 us -> 0 us
    pallas_call x0 -> x1, Pallas kernels: none -> 4.14 us  [local(): pl.pallas_call(functools.partial(order, (radix, m, n)), grid=(4,), out_sh...]
    unnamed x1 -> x0, local copies, waits for them, and re-layouts: 2.26 us -> none
    pallas_call x1, Pallas kernels: 62.9 us -> 62.1 us  [local(): pl.pallas_call(functools.partial(kernel, (steps, groups, nk, nz, rows, n,...]
where the time goes in v1:
time: 66.5 us; the launch traced here: 66.3 us
  Pallas kernels  66.3 us (100%)
    pallas_call x1, Pallas kernels, local(): pl.pallas_call(functools.partial(kernel, (steps, groups, nk, nz, rows, n,...  62.1 us
    pallas_call x1, Pallas kernels, local(): pl.pallas_call(functools.partial(order, (radix, m, n)), grid=(4,), out_sh...  4.14 us

profile of v1, /device:TPU:11, one launch (start us, length us, event | category | flops | bytes accessed | tf_op | source)
XLA Modules:
  0.0 66.3 jit_solution(8811025504044973951)
XLA Ops:
  0.0 62.1 %shard_map.64.total = f32[4,128,512]{2,1,0:T(8,128)} custom-call(s32[4]{0:T(128)} %owner_ref.1, f32[4]{0:T(128)} %weight_ref.1, f32[2,512,512]{2,1,0:T(8,128)} %bitcast.2, f32[2,2,64,512]{3,2,1,0:T(8,128)} %kern_hbm.1, bf16[4,512,256]{2,1,0:T(8,128)(2,1)} %constant.4.clone.rowt_hbm, bf16[4,256,512]{2,1,0:T(8,128)(2,1)} %constant.5.clone.colt_hbm), custom_call_target="tpu_custom_call" | custom-call | tf_op jit(solution)/shard_map/pallas_call | solution.py:246
  62.2 4.1 %shard_map.65 = f32[512,512]{1,0:T(8,128)} custom-call(f32[4,128,512]{2,1,0:T(8,128)} %shard_map.64.total), custom_call_target="tpu_custom_call" | custom-call | tf_op jit(solution)/shard_map/pallas_call | solution.py:264

commit v2 on v0

--- a/solution.py
+++ b/solution.py
@@ -141,20 +141,22 @@
         to_core(s, 1, 2 * xo + c, y)
         to_core(s, 2, g, yo)
 
-    def gather_rest(s):
+    def gather_turned(s):
         for d in range(nz):
             arrive(piece(s, 2 * xo + c, near(d), yo), d_recv.at[s, d])
         to_core(s, 3, 2 * xo + c, yo)
-        for kind, (q, yy) in enumerate([(2 * x + co, y), (2 * xo + co, y), (2 * x + co, yo), (2 * xo + co, yo)]):
-            arrive(line(s, q, yy), c_recv.at[s, kind])
-
-    def compute(s):
-        @pl.loop(0, 2 * nz)
-        def _(i):
+
+    def rows_in(s, yy):
+        for kind in (0, 1) if yy is y else (2, 3):
+            arrive(line(s, 2 * x + co if kind % 2 == 0 else 2 * xo + co, yy), c_recv.at[s, kind])
+
+        @pl.loop(0, nz)
+        def _(zi):
+            i = 2 * zi + yy
             at = pl.ds(pl.multiple_of(i * rows, rows), rows)
             re, im = [], []
             for q in range(groups):
-                kr, ki = held[s, q, 0, i // 2, i % 2], held[s, q, 1, i // 2, i % 2]
+                kr, ki = held[s, q, 0, zi, yy], held[s, q, 1, zi, yy]
                 mr, mi = mask[0, at, q * m:(q + 1) * m], mask[1, at, q * m:(q + 1) * m]
                 re.append(mr * kr - mi * ki)
                 im.append(mr * ki + mi * kr)
@@ -164,6 +166,10 @@
                     stage[r, at, p * m:(p + 1) * m] = hi
                     stage[r, at, (2 + p) * m:(3 + p) * m] = lo
 
+    def compute(s):
+        gather_turned(s)
+        rows_in(s, y)
+        rows_in(s, yo)
         for r in range(radix):
             hi, lo = stage[r, :, :2 * m], stage[r, :, 2 * m:]
             th, tl = rowt[r, :2 * m], rowt[r, 2 * m:]
@@ -207,9 +213,7 @@
             gather_z(s + 1)
         gather_xy(s)
         if s:
-            gather_rest(s - 1)
             compute(s - 1)
-    gather_rest(steps - 1)
     compute(steps - 1)
 
     for rx in range(radix):

time: 65.3 us -> 64.4 us (0.986)
  Pallas kernels: 62.9 us -> 61.9 us
    pallas_call x1, Pallas kernels: 62.9 us -> 61.9 us  [local(): pl.pallas_call(functools.partial(kernel, (steps, groups, nk, nz, rows, n,...]
where the time goes in v2:
time: 64.4 us; the launch traced here: 64.2 us
  Pallas kernels  61.9 us (96%)
  local copies, waits for them, and re-layouts  2.26 us (4%)
    pallas_call x1, Pallas kernels, local(): pl.pallas_call(functools.partial(kernel, (steps, groups, nk, nz, rows, n,...  61.9 us
    unnamed x1, local copies, waits for them, and re-layouts  2.26 us

profile of v2, /device:TPU:11, one launch (start us, length us, event | category | flops | bytes accessed | tf_op | source)
XLA Modules:
  0.0 64.2 jit_solution(9317424262586710436)
XLA Ops:
  0.0 61.9 %shard_map.64 = f32[512,512]{1,0:T(8,128)} custom-call(s32[4]{0:T(128)} %owner_ref.1, f32[4]{0:T(128)} %weight_ref.1, f32[2,512,512]{2,1,0:T(8,128)} %bitcast.3, f32[2,2,64,512]{3,2,1,0:T(8,128)} %kern_hbm.1, bf16[4,512,256]{2,1,0:T(8,128)(2,1)} %constant.4.clone.rowt_hbm, bf16[4,256,512]{2,1,0:T(8,128)(2,1)} %constant.5.clone.colt_hbm), custom_call_target="tpu_custom_call" | custom-call | tf_op jit(solution)/shard_map/pallas_call | solution.py:242
  61.9 2.3 %copy.8 = f32[1,512,512]{2,1,0:T(8,128)} copy(f32[1,512,512]{2,1,0:T(8,128)} %bitcast.2) | data formatting | bytes 2097152
